TPU v7x, 128 devices: a whole 4x4x4 slice. The times are simulated.
128 devices in a mesh: depth: 8 (over x, z_hi), screen: 16 (over z_lo, y, core).
Axes of the slice: x: 4, y: 4, z: 4 (z_hi: 2, z_lo: 2; z = z_hi * 2 + z_lo), core: 2. Of those that a mesh axis runs over, the one named last changes fastest.
Arguments:
- voxel_bins: int32 [64, 256, 4096], P('depth', None, 'screen'), may hold values from 0 to 255
- colors: bfloat16 [3, 256], replicated, may hold values from 0 to 2
- opacity: bfloat16 [256], replicated, may hold values from 0 to 1
- slab_order: int32 [16, 8], replicated, may hold values from 0 to 7, each once within a row
Outputs:
- image: float32 [4, 256, 4096], P(None, ('depth', 'screen'))
Inputs may be any that keep to these rules, and one draw needn't show every extreme that they name: `slab_order`: every row is a permutation of 0 to 7.
All inputs are finite; a program needn't handle non-finite values.
Results may differ from a plain program's by a relative error of at most 0.0003.
Values sent between devices are 32-bit elements; how exact they have to be, the bound alone decides.
A program may use at most 64 MiB of HBM per device.

v0:
```python
import math

import jax
import jax.numpy as jnp
from jax import lax
from jax.sharding import PartitionSpec as P

low_count = 16
extinction = 3.0


def look_up(table_rows, bin_block):
    high_count = table_rows.shape[0] // 4
    low_part = bin_block % low_count
    high_part = bin_block // low_count
    low_onehot = (low_part[None, :] == jnp.arange(low_count, dtype=jnp.int32)[:, None]).astype(
        jnp.bfloat16
    )
    picked = jnp.dot(table_rows, low_onehot, preferred_element_type=jnp.float32)
    picked = picked.reshape(4, high_count, bin_block.shape[0])
    high_match = high_part[None, :] == jnp.arange(high_count, dtype=jnp.int32)[:, None]
    return jnp.sum(jnp.where(high_match[None], picked, 0.0), axis=1)


def render(voxel_bins, table_rows, total_samples):
    samples_here, row_count, col_count = voxel_bins.shape
    pixels = row_count * col_count
    per_step = math.gcd(samples_here, max(1, 131072 // pixels))
    blocks = voxel_bins.reshape(samples_here // per_step, per_step * pixels)
    extinct_rate = extinction / total_samples

    def advance(carried, bin_block):
        passed, color_sum = carried
        values = look_up(table_rows, bin_block).reshape(4, per_step, pixels)
        density = values[3]
        before = jnp.cumsum(density, axis=0) - density
        weight = (1.0 - jnp.exp(-extinct_rate * density)) * jnp.exp(
            -extinct_rate * (passed[None] + before)
        )
        color_sum = color_sum + jnp.sum(weight[None] * values[:3], axis=1)
        return ((passed + jnp.sum(density, axis=0), color_sum), None)

    start = (jnp.zeros((pixels,), jnp.float32), jnp.zeros((3, pixels), jnp.float32))
    (passed, color_sum), ignored = lax.scan(advance, start, blocks)
    final_alpha = 1.0 - jnp.exp(-extinct_rate * passed)
    partial_value = jnp.concatenate([color_sum, final_alpha[None]], axis=0)
    return partial_value.reshape(4, row_count, col_count)


def composite(pieces, places):
    in_front = (places[:, None, :] < places[:, :, None]).astype(jnp.float32)
    clear_log = jnp.log1p(-pieces[:, :, 3])
    front_log = jnp.einsum("tij,jtrw->itrw", in_front, clear_log, precision=lax.Precision.HIGHEST)
    shaded = jnp.sum(pieces[:, :, :3] * jnp.exp(front_log)[:, :, None], axis=0)
    total_alpha = 1.0 - jnp.exp(jnp.sum(clear_log, axis=0))
    merged = jnp.concatenate([shaded, total_alpha[:, None]], axis=1)
    return jnp.transpose(merged, (1, 2, 0, 3))


def local(voxel_bins, colors, opacity, slab_order):
    table = jnp.concatenate([colors, opacity[None]], axis=0)
    table_rows = table.reshape(4 * (table.shape[1] // low_count), low_count)
    depth_count = lax.axis_size("depth")
    screen_count = lax.axis_size("screen")
    total_samples = voxel_bins.shape[0] * depth_count
    partial_value = render(voxel_bins, table_rows, total_samples)
    row_count = partial_value.shape[1]
    col_count = partial_value.shape[2]
    owned_rows = row_count // (depth_count * screen_count)
    pieces = lax.all_to_all(
        partial_value[None], ("depth", "screen"), split_axis=2, concat_axis=0, tiled=True
    )
    ordered = pieces.reshape(depth_count, screen_count, 4, pieces.shape[2], pieces.shape[3])
    joined = composite(ordered, slab_order)
    result = joined.reshape(4, owned_rows, screen_count * col_count)
    return result


def solution(mesh):
    placed = (P("depth", None, "screen"), P(), P(), P())
    return jax.shard_map(
        local,
        mesh=mesh,
        in_specs=placed,
        out_specs=P(None, ("depth", "screen"), None),
        check_vma=False,
    )
```

profile of v0, /device:TPU:1, one launch (start us, length us, event | category | flops | bytes accessed | tf_op | source)
XLA Modules:
  0.0 180.9 jit_solution(15716639711246271932)
XLA Ops:
  0.0 4.0 %reshape.117 = s32[4,131072]{1,0:T(4,128)} reshape(s32[8,256,256]{2,1,0:T(8,128)} %param.6) | data formatting | bytes 4194304 | tf_op jit(solution)/shard_map/reshape | solution.py:29
  4.2 140.2 %while.15 = (s32[]{:T(128)}, f32[65536]{0:T(1024)}, f32[3,65536]{1,0:T(4,128)}, s32[4,131072]{1,0:T(4,128)}, bf16[64,16]{0,1:T(8,128)(2,1)S(1)}, /*index=5*/s32[]{:T(128)}, f32[]{:T(128)}, s32[]{:T(128)}) while((s32[]{:T(128)}, f32[65536]{0:T(1024)}, f32[3,65536]{1,0:T(4,128)}, s32[4,131072]{1,0:T(4,128)}, ...), condition=%wide.region_5.6_spmd.clone, body=%wide.region_0.5_spmd.clone.sunk | while | flops 293994496 | bytes 31983784 | solution.py:44
  4.2 3.4 %and_select_fusion.4 = (s32[1,131072]{1,0:T(1,128)S(1)}, s32[1,131072]{1,0:T(1,128)S(1)}) fusion(s32[4,131072]{1,0:T(4,128)} %get-tuple-element.186, s32[]{:T(128)} %get-tuple-element.175), kind=kLoop, calls=%fused_computation.5.clone.1 | loop fusion | flops 1441792 | bytes 1572868 | tf_op jit(solution)/shard_map/while/body/eval_jaxpr/jit(remainder)/select_n | solution.py:14
  7.6 3.8 %and_select_fusion.5 = s32[1,131072]{1,0:T(1,128)S(1)} fusion(s32[1,131072]{1,0:T(1,128)S(1)} %get-tuple-element.163, s32[4,131072]{1,0:T(4,128)} %get-tuple-element.186, s32[]{:T(128)} %get-tuple-element.175), kind=kLoop, calls=%fused_computation.6.clone.1 | loop fusion | flops 1572864 | bytes 1572868 | tf_op jit(solution)/shard_map/while/body/eval_jaxpr/jit(floor_divide)/jit(_where)/select_n | solution.py:15
  12.5 11.0 %select_reduce_fusion.2 = f32[4,131072]{1,0:T(4,128)S(1)} fusion(pred[16,131072]{1,0:T(8,128)(4,1)S(1)} %iota_compare_fusion.4, bf16[64,16]{0,1:T(8,128)(2,1)S(1)} %get-tuple-element.187, s32[131072]{0:T(1024)S(1)} %bitcast.42), kind=kOutput, calls=%fused_computation.clone.1 | convolution fusion | flops 286785536 | bytes 4720640 | tf_op jit(solution)/shard_map/while/body/eval_jaxpr/dot_general | solution.py:19
  26.7 1.8 %reduce_window_sum.13 = f32[2,65536]{1,0:T(2,128)} reduce-window(f32[2,65536]{1,0:T(2,128)S(1)} %squeeze.11, f32[]{:T(128)} %constant.75.clone.7..sunk), window={size=2x1 pad=1_0x0_0}, to_apply=%region_3.3 | reduce-window | flops 131072 | bytes 1048580 | tf_op jit(solution)/shard_map/while/body/eval_jaxpr/jit(cumsum)/reduce_window_sum | solution.py:36
  28.5 1.8 exponential_multiply_fusion.2
  30.3 2.9 %slice.38 = f32[3,2,65536]{2,1,0:T(2,128)} reshape(f32[3,131072]{1,0:T(4,128)S(1)} %bitcast.40) | data formatting | bytes 3145728 | tf_op jit(solution)/shard_map/while/body/eval_jaxpr/slice | solution.py:40
  33.1 3.9 %multiply_reduce_fusion.2 = f32[3,65536]{1,0:T(4,128)S(1)} fusion(f32[3,2,65536]{2,1,0:T(2,128)} %slice.38, f32[2,65536]{1,0:T(2,128)S(1)} %exponential_multiply_fusion.2), kind=kLoop, calls=%fused_computation.7.clone.1 | loop fusion | flops 589824 | bytes 2883584 | tf_op jit(solution)/shard_map/while/body/eval_jaxpr/reduce_sum | solution.py:40
  38.6 3.4 %and_select_fusion.4 = (s32[1,131072]{1,0:T(1,128)S(1)}, s32[1,131072]{1,0:T(1,128)S(1)}) fusion(s32[4,131072]{1,0:T(4,128)} %get-tuple-element.186, s32[]{:T(128)} %get-tuple-element.175), kind=kLoop, calls=%fused_computation.5.clone.1 | loop fusion | flops 1441792 | bytes 1572868 | tf_op jit(solution)/shard_map/while/body/eval_jaxpr/jit(remainder)/select_n | solution.py:14
  41.9 3.8 %and_select_fusion.5 = s32[1,131072]{1,0:T(1,128)S(1)} fusion(s32[1,131072]{1,0:T(1,128)S(1)} %get-tuple-element.163, s32[4,131072]{1,0:T(4,128)} %get-tuple-element.186, s32[]{:T(128)} %get-tuple-element.175), kind=kLoop, calls=%fused_computation.6.clone.1 | loop fusion | flops 1572864 | bytes 1572868 | tf_op jit(solution)/shard_map/while/body/eval_jaxpr/jit(floor_divide)/jit(_where)/select_n | solution.py:15
  46.8 11.0 %select_reduce_fusion.2 = f32[4,131072]{1,0:T(4,128)S(1)} fusion(pred[16,131072]{1,0:T(8,128)(4,1)S(1)} %iota_compare_fusion.4, bf16[64,16]{0,1:T(8,128)(2,1)S(1)} %get-tuple-element.187, s32[131072]{0:T(1024)S(1)} %bitcast.42), kind=kOutput, calls=%fused_computation.clone.1 | convolution fusion | flops 286785536 | bytes 4720640 | tf_op jit(solution)/shard_map/while/body/eval_jaxpr/dot_general | solution.py:19
  62.0 1.8 %reduce_window_sum.13 = f32[2,65536]{1,0:T(2,128)} reduce-window(f32[2,65536]{1,0:T(2,128)S(1)} %squeeze.11, f32[]{:T(128)} %constant.75.clone.7..sunk), window={size=2x1 pad=1_0x0_0}, to_apply=%region_3.3 | reduce-window | flops 131072 | bytes 1048580 | tf_op jit(solution)/shard_map/while/body/eval_jaxpr/jit(cumsum)/reduce_window_sum | solution.py:36
  63.8 1.8 exponential_multiply_fusion.2
  65.6 2.9 %slice.38 = f32[3,2,65536]{2,1,0:T(2,128)} reshape(f32[3,131072]{1,0:T(4,128)S(1)} %bitcast.40) | data formatting | bytes 3145728 | tf_op jit(solution)/shard_map/while/body/eval_jaxpr/slice | solution.py:40
  68.4 3.9 %multiply_reduce_fusion.2 = f32[3,65536]{1,0:T(4,128)S(1)} fusion(f32[3,2,65536]{2,1,0:T(2,128)} %slice.38, f32[2,65536]{1,0:T(2,128)S(1)} %exponential_multiply_fusion.2), kind=kLoop, calls=%fused_computation.7.clone.1 | loop fusion | flops 589824 | bytes 2883584 | tf_op jit(solution)/shard_map/while/body/eval_jaxpr/reduce_sum | solution.py:40
  73.9 3.4 %and_select_fusion.4 = (s32[1,131072]{1,0:T(1,128)S(1)}, s32[1,131072]{1,0:T(1,128)S(1)}) fusion(s32[4,131072]{1,0:T(4,128)} %get-tuple-element.186, s32[]{:T(128)} %get-tuple-element.175), kind=kLoop, calls=%fused_computation.5.clone.1 | loop fusion | flops 1441792 | bytes 1572868 | tf_op jit(solution)/shard_map/while/body/eval_jaxpr/jit(remainder)/select_n | solution.py:14
  77.2 3.8 %and_select_fusion.5 = s32[1,131072]{1,0:T(1,128)S(1)} fusion(s32[1,131072]{1,0:T(1,128)S(1)} %get-tuple-element.163, s32[4,131072]{1,0:T(4,128)} %get-tuple-element.186, s32[]{:T(128)} %get-tuple-element.175), kind=kLoop, calls=%fused_computation.6.clone.1 | loop fusion | flops 1572864 | bytes 1572868 | tf_op jit(solution)/shard_map/while/body/eval_jaxpr/jit(floor_divide)/jit(_where)/select_n | solution.py:15
  82.1 11.0 %select_reduce_fusion.2 = f32[4,131072]{1,0:T(4,128)S(1)} fusion(pred[16,131072]{1,0:T(8,128)(4,1)S(1)} %iota_compare_fusion.4, bf16[64,16]{0,1:T(8,128)(2,1)S(1)} %get-tuple-element.187, s32[131072]{0:T(1024)S(1)} %bitcast.42), kind=kOutput, calls=%fused_computation.clone.1 | convolution fusion | flops 286785536 | bytes 4720640 | tf_op jit(solution)/shard_map/while/body/eval_jaxpr/dot_general | solution.py:19
  97.2 1.8 %reduce_window_sum.13 = f32[2,65536]{1,0:T(2,128)} reduce-window(f32[2,65536]{1,0:T(2,128)S(1)} %squeeze.11, f32[]{:T(128)} %constant.75.clone.7..sunk), window={size=2x1 pad=1_0x0_0}, to_apply=%region_3.3 | reduce-window | flops 131072 | bytes 1048580 | tf_op jit(solution)/shard_map/while/body/eval_jaxpr/jit(cumsum)/reduce_window_sum | solution.py:36
  99.1 1.8 exponential_multiply_fusion.2
  100.8 2.9 %slice.38 = f32[3,2,65536]{2,1,0:T(2,128)} reshape(f32[3,131072]{1,0:T(4,128)S(1)} %bitcast.40) | data formatting | bytes 3145728 | tf_op jit(solution)/shard_map/while/body/eval_jaxpr/slice | solution.py:40
  103.7 3.9 %multiply_reduce_fusion.2 = f32[3,65536]{1,0:T(4,128)S(1)} fusion(f32[3,2,65536]{2,1,0:T(2,128)} %slice.38, f32[2,65536]{1,0:T(2,128)S(1)} %exponential_multiply_fusion.2), kind=kLoop, calls=%fused_computation.7.clone.1 | loop fusion | flops 589824 | bytes 2883584 | tf_op jit(solution)/shard_map/while/body/eval_jaxpr/reduce_sum | solution.py:40
  109.1 3.4 %and_select_fusion.4 = (s32[1,131072]{1,0:T(1,128)S(1)}, s32[1,131072]{1,0:T(1,128)S(1)}) fusion(s32[4,131072]{1,0:T(4,128)} %get-tuple-element.186, s32[]{:T(128)} %get-tuple-element.175), kind=kLoop, calls=%fused_computation.5.clone.1 | loop fusion | flops 1441792 | bytes 1572868 | tf_op jit(solution)/shard_map/while/body/eval_jaxpr/jit(remainder)/select_n | solution.py:14
  112.5 3.8 %and_select_fusion.5 = s32[1,131072]{1,0:T(1,128)S(1)} fusion(s32[1,131072]{1,0:T(1,128)S(1)} %get-tuple-element.163, s32[4,131072]{1,0:T(4,128)} %get-tuple-element.186, s32[]{:T(128)} %get-tuple-element.175), kind=kLoop, calls=%fused_computation.6.clone.1 | loop fusion | flops 1572864 | bytes 1572868 | tf_op jit(solution)/shard_map/while/body/eval_jaxpr/jit(floor_divide)/jit(_where)/select_n | solution.py:15
  117.4 11.0 %select_reduce_fusion.2 = f32[4,131072]{1,0:T(4,128)S(1)} fusion(pred[16,131072]{1,0:T(8,128)(4,1)S(1)} %iota_compare_fusion.4, bf16[64,16]{0,1:T(8,128)(2,1)S(1)} %get-tuple-element.187, s32[131072]{0:T(1024)S(1)} %bitcast.42), kind=kOutput, calls=%fused_computation.clone.1 | convolution fusion | flops 286785536 | bytes 4720640 | tf_op jit(solution)/shard_map/while/body/eval_jaxpr/dot_general | solution.py:19
  132.5 1.8 %reduce_window_sum.13 = f32[2,65536]{1,0:T(2,128)} reduce-window(f32[2,65536]{1,0:T(2,128)S(1)} %squeeze.11, f32[]{:T(128)} %constant.75.clone.7..sunk), window={size=2x1 pad=1_0x0_0}, to_apply=%region_3.3 | reduce-window | flops 131072 | bytes 1048580 | tf_op jit(solution)/shard_map/while/body/eval_jaxpr/jit(cumsum)/reduce_window_sum | solution.py:36
  136.1 2.9 %slice.38 = f32[3,2,65536]{2,1,0:T(2,128)} reshape(f32[3,131072]{1,0:T(4,128)S(1)} %bitcast.40) | data formatting | bytes 3145728 | tf_op jit(solution)/shard_map/while/body/eval_jaxpr/slice | solution.py:40
  139.0 3.9 %multiply_reduce_fusion.2 = f32[3,65536]{1,0:T(4,128)S(1)} fusion(f32[3,2,65536]{2,1,0:T(2,128)} %slice.38, f32[2,65536]{1,0:T(2,128)S(1)} %exponential_multiply_fusion.2), kind=kLoop, calls=%fused_computation.7.clone.1 | loop fusion | flops 589824 | bytes 2883584 | tf_op jit(solution)/shard_map/while/body/eval_jaxpr/reduce_sum | solution.py:40
  145.4 2.7 %pad_maximum_fusion = f32[1,4,256,256]{3,1,0,2:T(4,128)} fusion(f32[1,1,256,256]{3,1,0,2:T(1,128)S(1)} %bitcast.47, f32[1,3,256,256]{3,1,0,2:T(4,128)} %bitcast.43), kind=kLoop, calls=%fused_computation.17 | loop fusion | flops 262144 | bytes 2097152 | tf_op jit(solution)/shard_map/concatenate | solution.py:46
  148.1 11.5 %all-to-all-start = ((f32[1,4,256,256]{3,1,0,2:T(4,128)}), f32[1,4,256,256]{3,1,0,2:T(4,128)S(1)}, u32[]{:S(2)}, u32[]{:S(2)}) async-start(f32[1,4,256,256]{3,1,0,2:T(4,128)} %pad_maximum_fusion), calls=%async_computation | async-start | bytes 2097152 | tf_op jit(solution)/shard_map/all_to_all | solution.py:70
  159.7 18.9 %all-to-all-done = f32[1,4,256,256]{3,1,0,2:T(4,128)S(1)} async-done(((f32[1,4,256,256]{3,1,0,2:T(4,128)}), f32[1,4,256,256]{3,1,0,2:T(4,128)S(1)}, u32[]{:S(2)}, u32[]{:S(2)}) %all-to-all-start) | async-done | bytes 1048608 | tf_op jit(solution)/shard_map/all_to_all | solution.py:70
  (65 shorter events, 31.5 us)
Async XLA Ops:
  0.0 4.0 %copy-start.4 = (bf16[256]{0:T(256)(128)(2,1)S(1)}, bf16[256]{0:T(256)(128)(2,1)}, u32[]{:S(2)}) copy-start(bf16[256]{0:T(256)(128)(2,1)} %param.8) | copy-start | bytes 1540
  0.0 4.0 %copy-start.3 = (bf16[3,256]{1,0:T(4,128)(2,1)S(1)}, bf16[3,256]{1,0:T(4,128)(2,1)}, u32[]{:S(2)}) copy-start(bf16[3,256]{1,0:T(4,128)(2,1)} %param.7) | copy-start | bytes 4612
  33.1 3.9 %copy-start = (f32[3,65536]{1,0:T(4,128)S(1)}, f32[3,65536]{1,0:T(4,128)}, u32[]{:S(2)}) copy-start(f32[3,65536]{1,0:T(4,128)} %get-tuple-element.177) | copy-start | bytes 2359300 | tf_op jit(solution)/shard_map/while
  37.6 1.0 copy-start.1
  68.4 3.9 %copy-start = (f32[3,65536]{1,0:T(4,128)S(1)}, f32[3,65536]{1,0:T(4,128)}, u32[]{:S(2)}) copy-start(f32[3,65536]{1,0:T(4,128)} %get-tuple-element.177) | copy-start | bytes 2359300 | tf_op jit(solution)/shard_map/while
  72.9 1.0 copy-start.1
  103.7 3.9 %copy-start = (f32[3,65536]{1,0:T(4,128)S(1)}, f32[3,65536]{1,0:T(4,128)}, u32[]{:S(2)}) copy-start(f32[3,65536]{1,0:T(4,128)} %get-tuple-element.177) | copy-start | bytes 2359300 | tf_op jit(solution)/shard_map/while
  108.2 1.0 copy-start.1
  139.0 3.9 %copy-start = (f32[3,65536]{1,0:T(4,128)S(1)}, f32[3,65536]{1,0:T(4,128)}, u32[]{:S(2)}) copy-start(f32[3,65536]{1,0:T(4,128)} %get-tuple-element.177) | copy-start | bytes 2359300 | tf_op jit(solution)/shard_map/while
  143.5 1.0 copy-start.1
  145.4 14.2 %copy-start.2 = (s32[16,8]{0,1:T(8,128)S(1)}, s32[16,8]{0,1:T(8,128)}, u32[]{:S(2)}) copy-start(s32[16,8]{0,1:T(8,128)} %param.9) | copy-start | bytes 1540
  148.1 30.5 %all-to-all-start = ((f32[1,4,256,256]{3,1,0,2:T(4,128)}), f32[1,4,256,256]{3,1,0,2:T(4,128)S(1)}, u32[]{:S(2)}, u32[]{:S(2)}) async-start(f32[1,4,256,256]{3,1,0,2:T(4,128)} %pad_maximum_fusion), calls=%async_computation | async-start | bytes 2097152 | tf_op jit(solution)/shard_map/all_to_all | solution.py:70
where the time goes:
time: 182 us; the launch traced here: 181 us
  other arithmetic  77.5 us (43%)
  matrix products  44.4 us (24%)
  local copies, waits for them, and re-layouts  28.1 us (15%)
  waiting for transfers between devices  18.9 us (10%)
  starting transfers between devices  11.5 us (6%)
    dot_general x4, matrix products, look_up(): picked = jnp.dot(table_rows, low_onehot, preferred_element_type=jnp.float32)  44 us
    all_to_all x1, waiting for transfers between devices, local(): lax.all_to_all(partial_value[None], ('depth', 'screen'), split_axis=2, co...  18.9 us
    reduce_sum x4, other arithmetic, advance(): color_sum = color_sum + jnp.sum(weight[None] * values[:3], axis=1)  15.4 us
    select_n x4, other arithmetic, look_up(): high_part = bin_block // low_count  15 us
    select_n x4, other arithmetic, look_up(): low_part = bin_block % low_count  13.5 us
    all_to_all x1, starting transfers between devices, local(): lax.all_to_all(partial_value[None], ('depth', 'screen'), split_axis=2, co...  11.5 us
    slice x4, local copies, waits for them, and re-layouts, advance(): color_sum = color_sum + jnp.sum(weight[None] * values[:3], axis=1)  11.4 us
    another operation x4, other arithmetic, advance(): before = jnp.cumsum(density, axis=0) - density  7.29 us
  transfers between devices with their start and end apart: 1, of which 1 were waited for; matrix products, arithmetic and copies ran while one was open for 0% of the time, Pallas kernels for 0%

commit v1 on v0

v1 whole, which is shorter than its diff:
```python
import jax
import jax.numpy as jnp
from jax import lax
from jax.experimental import pallas as pl
from jax.experimental.pallas import tpu as pltpu
from jax.sharding import PartitionSpec as P

extinction = 3.0
MESH = pl.DeviceIdType.MESH


def ring(step):
    return min(step, 4 - step)


OFFSETS = sorted(
    [(dx, dz) for dx in range(4) for dz in range(4) if (dx, dz) != (0, 0)],
    key=lambda o: (-(ring(o[0]) + ring(o[1])), (o[0] * 5 + o[1] * 3) % 11),
)
PEERS = len(OFFSETS)
NEAR = [(2, 0), (2, 1), (3, 0), (3, 1), (1, 0), (1, 1), (0, 1)]
SLOTS = len(NEAR)


def coords():
    depth = lax.axis_index("depth")
    screen = lax.axis_index("screen")
    return depth // 2, (depth % 2) * 2 + screen // 8, (screen // 2) % 4, screen % 2


def device(x, z, y, core):
    return {"depth": x * 2 + z // 2, "screen": (z % 2) * 8 + y * 2 + core}


def gather_lanes(table, lanes):
    return jnp.take_along_axis(table, lanes, axis=1, mode="promise_in_bounds")


def shade(bins, tables):
    sums = None
    for layer in bins:
        lanes = layer & 127
        low = layer < 128
        values = [
            jnp.where(low, gather_lanes(tables[2 * ch], lanes), gather_lanes(tables[2 * ch + 1], lanes))
            for ch in range(4)
        ]
        if sums is None:
            sums = values
        else:
            clear = 1.0 - sums[3]
            sums = [s + clear * v for s, v in zip(sums, values)]
    return sums


def regroup(planes, pair):
    low_half = pair < 2
    even = (pair % 2) == 0
    u0 = jnp.where(low_half, planes[0], pltpu.roll(planes[2], 4, 0))
    u1 = jnp.where(low_half, planes[1], pltpu.roll(planes[3], 4, 0))
    v0 = jnp.where(low_half, pltpu.roll(planes[0], 4, 0), planes[2])
    v1 = jnp.where(low_half, pltpu.roll(planes[1], 4, 0), planes[3])
    return [
        jnp.where(even, u0, pltpu.roll(u1, 2, 0)),
        jnp.where(even, pltpu.roll(u0, 6, 0), u1),
        jnp.where(even, v0, pltpu.roll(v1, 2, 0)),
        jnp.where(even, pltpu.roll(v0, 6, 0), v1),
    ]


def kernel(
    vox, table_ref, order_ref, out_ref,
    vin, send_far, send_near, recv_far, recv_sib, recv_other, recv_own, result, landed, place,
    load_sem, self_sem, send_sem, recv_sem, send2_sem, recv2_sem,
):
    x, z, y, core = coords()
    half = y // 2
    me_block = x * 4 + z
    slab = x * 2 + z // 2
    side = z % 2
    sibling = y + 1 - 2 * (y % 2)
    ys = [y, sibling, (y + 2) % 4, (sibling + 2) % 4]
    cores = [core, 1 - core]

    def load(part):
        source = half if part else 1 - half
        return pltpu.make_async_copy(vox.at[:, :, source], vin.at[part], load_sem.at[part])

    load(0).start()
    load(1).start()

    barrier = pltpu.get_barrier_semaphore()
    for dx, dz in OFFSETS:
        pl.semaphore_signal(
            barrier, inc=1, device_id=device((x + dx) % 4, (z + dz) % 4, y, core), device_id_type=MESH
        )
    for yrel, crel in NEAR:
        pl.semaphore_signal(barrier, inc=1, device_id=device(x, z, ys[yrel], cores[crel]), device_id_type=MESH)

    for t in range(2):
        row = t * 8 + y * 2 + core
        places = [order_ref[i, row] for i in range(8)]
        for k in range(8):
            found = jnp.int32(0)
            for i in range(8):
                found = jnp.where(places[i] == k, jnp.int32(i), found)
            place[t * 8 + k] = found

    tables = [jnp.broadcast_to(table_ref[i : i + 1, :], (8, 128)) for i in range(8)]
    pair = lax.broadcasted_iota(jnp.int32, (8, 128), 0) // 2

    def render(part):
        def rows(step, carry):
            for sub in range(2):
                block = step * 2 + sub
                for col in range(2):
                    span = pl.ds(col * 128, 128)
                    bins = [vin[part, j, block, :, span] for j in range(8)]
                    blocks = regroup(shade(bins, tables), pair)
                    for q in range(4):
                        if part == 0:
                            send_far[block, q // 2, q % 2, :, span] = blocks[q]
                        else:
                            send_near[(q // 2 + y) % 2, block, q % 2, :, span] = blocks[q]
            return carry

        lax.fori_loop(0, 8, rows, 0)

    buffers = [
        (lambda b: send_far.at[b], recv_far),
        (lambda b: send_near.at[1, b], recv_sib),
        (lambda b: send_near.at[0, b, 1 - core], recv_other),
        (lambda b: send_near.at[0, b, core], recv_own),
    ]

    def message(group, k):
        dx, dz = OFFSETS[k]
        to_x, to_z = (x + dx) % 4, (z + dz) % 4
        source, target = buffers[group]
        return pltpu.make_async_remote_copy(
            src_ref=source(to_x * 4 + to_z),
            dst_ref=target.at[side, slab],
            send_sem=send_sem.at[group, k],
            recv_sem=recv_sem.at[group, k],
            device_id=device(to_x, to_z, y, core),
            device_id_type=MESH,
        )

    def keep(group):
        source, target = buffers[group]
        return pltpu.make_async_copy(source(me_block), target.at[side, slab], self_sem.at[group])

    def send(group):
        for k in range(PEERS):
            message(group, k).start()
        keep(group).start()

    def arrive(group):
        for k in range(PEERS):
            message(group, k).wait_recv()
        keep(group).wait()

    load(0).wait()
    render(0)
    pl.semaphore_wait(barrier, PEERS + SLOTS)
    send(0)
    load(1).wait()
    render(1)
    send(1)
    send(2)
    send(3)

    alpha_rows = 6 + lax.broadcasted_iota(jnp.int32, (8, 128), 0) % 2

    def over(read, store):
        for t in range(2):
            for col in range(2):
                span = pl.ds(col * 128, 128)
                total = read(t, place[t * 8], span)
                for k in range(1, 8):
                    alpha = jnp.take_along_axis(total, alpha_rows, axis=0, mode="promise_in_bounds")
                    total = total + (1.0 - alpha) * read(t, place[t * 8 + k], span)
                store(t, span, total)

    def forward(slot):
        yrel, crel = NEAR[slot]
        return pltpu.make_async_remote_copy(
            src_ref=result.at[slot],
            dst_ref=landed.at[slot],
            send_sem=send2_sem.at[slot],
            recv_sem=recv2_sem.at[slot],
            device_id=device(x, z, ys[yrel], cores[crel]),
            device_id_type=MESH,
        )

    def pass_on(slot, read):
        def store(t, span, total):
            result[slot, t, :, span] = total

        over(read, store)
        forward(slot).start()

    arrive(0)
    for slot in range(4):
        yrel, crel = NEAR[slot]
        pass_on(slot, lambda t, s, span: recv_far[t, s, ys[yrel] % 2, cores[crel], :, span])
    arrive(1)
    for slot in range(4, 6):
        crel = NEAR[slot][1]
        pass_on(slot, lambda t, s, span: recv_sib[t, s, cores[crel], :, span])
    arrive(2)
    pass_on(6, lambda t, s, span: recv_other[t, s, :, span])

    def put(slot):
        yrel, crel = NEAR[slot]
        forward(slot).wait_recv()
        for t in range(2):
            out_ref[t * 8 + ys[yrel] * 2 + cores[crel]] = landed[slot, t]

    for slot in range(4):
        put(slot)
    arrive(3)

    def store_own(t, span, total):
        out_ref[t * 8 + y * 2 + core, :, span] = total

    over(lambda t, s, span: recv_own[t, s, :, span], store_own)
    for slot in range(4, SLOTS):
        put(slot)

    for group in range(4):
        for k in range(PEERS):
            message(group, k).wait_send()
    for slot in range(SLOTS):
        forward(slot).wait_send()


def local(voxel_bins, colors, opacity, slab_order):
    rate = extinction / (voxel_bins.shape[0] * lax.axis_size("depth"))
    alpha = -jnp.expm1(-rate * opacity.astype(jnp.float32))
    shaded = jnp.concatenate([colors.astype(jnp.float32) * alpha[None], alpha[None]], axis=0)
    table = shaded.reshape(8, 128)
    vox = voxel_bins.reshape(8, 16, 2, 8, 256)
    f32 = jnp.float32
    out = pl.pallas_call(
        kernel,
        out_shape=jax.ShapeDtypeStruct((16, 8, 256), f32),
        in_specs=[
            pl.BlockSpec(memory_space=pl.ANY),
            pl.BlockSpec(memory_space=pltpu.VMEM),
            pl.BlockSpec(memory_space=pltpu.SMEM),
        ],
        out_specs=pl.BlockSpec(memory_space=pltpu.VMEM),
        scratch_shapes=[
            pltpu.VMEM((2, 8, 16, 8, 256), jnp.int32),
            pltpu.VMEM((16, 2, 2, 8, 256), f32),
            pltpu.VMEM((2, 16, 2, 8, 256), f32),
            pltpu.VMEM((2, 8, 2, 2, 8, 256), f32),
            pltpu.VMEM((2, 8, 2, 8, 256), f32),
            pltpu.VMEM((2, 8, 8, 256), f32),
            pltpu.VMEM((2, 8, 8, 256), f32),
            pltpu.VMEM((SLOTS, 2, 8, 256), f32),
            pltpu.VMEM((SLOTS, 2, 8, 256), f32),
            pltpu.SMEM((16,), jnp.int32),
            pltpu.SemaphoreType.DMA((2,)),
            pltpu.SemaphoreType.DMA((4,)),
            pltpu.SemaphoreType.DMA((4, PEERS)),
            pltpu.SemaphoreType.DMA((4, PEERS)),
            pltpu.SemaphoreType.DMA((SLOTS,)),
            pltpu.SemaphoreType.DMA((SLOTS,)),
        ],
        compiler_params=pltpu.CompilerParams(collective_id=0, has_side_effects=True),
        name="render_exchange",
    )(vox, table, slab_order.T)
    out = out.reshape(16, 4, 2, 256)
    return jnp.transpose(out, (1, 2, 0, 3)).reshape(4, 2, 4096)


def solution(mesh):
    placed = (P("depth", None, "screen"), P(), P(), P())
    return jax.shard_map(
        local,
        mesh=mesh,
        in_specs=placed,
        out_specs=P(None, ("depth", "screen"), None),
        check_vma=False,
    )
```

time: 182 us -> 31.7 us (0.17)
  other arithmetic: 77.5 us -> 1.36 us
  matrix products: 44.4 us -> 0 us
  Pallas kernels: 0 us -> 27.8 us
  local copies, waits for them, and re-layouts: 28.1 us -> 2.26 us
  waiting for transfers between devices: 18.9 us -> 0 us
  starting transfers between devices: 11.5 us -> 0 us
    dot_general x5 -> x0, matrix products: 44.4 us -> none  [the longest x4 44 us: look_up(): picked = jnp.dot(table_rows, low_onehot, preferred_element_type=jnp.float32)]
    select_n x8 -> x0, other arithmetic: 28.5 us -> none  [the longest x4 15 us: look_up(): high_part = bin_block // low_count]
    pallas_call x0 -> x1, Pallas kernels: none -> 27.8 us  [local(): pl.pallas_call(kernel, out_shape=jax.ShapeDtypeStruct((16, 8, 256), f32),...]
    all_to_all x1 -> x0, waiting for transfers between devices: 18.9 us -> none  [local(): lax.all_to_all(partial_value[None], ('depth', 'screen'), split_axis=2, co...]
    reduce_sum x10 -> x0, other arithmetic: 18.3 us -> none  [the longest x4 15.4 us: advance(): color_sum = color_sum + jnp.sum(weight[None] * values[:3], axis=1)]
    slice x9 -> x0, local copies, waits for them, and re-layouts: 17.5 us -> none  [the longest x4 11.4 us: advance(): color_sum = color_sum + jnp.sum(weight[None] * values[:3], axis=1)]
    all_to_all x1 -> x0, starting transfers between devices: 11.5 us -> none  [local(): lax.all_to_all(partial_value[None], ('depth', 'screen'), split_axis=2, co...]
    add x8 -> x0, other arithmetic: 8.33 us -> none  [the longest x4 5.85 us: advance(): return ((passed + jnp.sum(density, axis=0), color_sum), None)]
  transfers between devices with their start and end apart: 1 -> 0, of which waited for: 1 -> 0; matrix products, arithmetic and copies ran while one was open for 0% -> 0% of each run, Pallas kernels for 0% -> 0%
where the time goes in v1:
time: 31.7 us; the launch traced here: 31.4 us
  Pallas kernels  27.8 us (88%)
  local copies, waits for them, and re-layouts  2.26 us (7%)
  other arithmetic  1.36 us (4%)
    pallas_call x1, Pallas kernels, local(): pl.pallas_call(kernel, out_shape=jax.ShapeDtypeStruct((16, 8, 256), f32),...  27.8 us
    reshape x1, local copies, waits for them, and re-layouts, local(): out = out.reshape(16, 4, 2, 256)  0.98 us
    mul x1, other arithmetic, local(): colors.astype(jnp.float32) * alpha[None]  0.69 us
    reshape x1, local copies, waits for them, and re-layouts, local(): return jnp.transpose(out, (1, 2, 0, 3)).reshape(4, 2, 4096)  0.68 us
    neg x1, other arithmetic, local(): alpha = -jnp.expm1(-rate * opacity.astype(jnp.float32))  0.66 us

profile of v1, /device:TPU:1, one launch (start us, length us, event | category | flops | bytes accessed | tf_op | source)
XLA Modules:
  0.0 31.4 jit_solution(15264825213979101295)
XLA Ops:
  0.0 0.7 %exponential-minus-one_negate_fusion = f32[256]{0:T(256)S(1)} fusion(bf16[256]{0:T(256)(128)(2,1)} %param.6), kind=kLoop, calls=%fused_computation.2 | loop fusion | flops 768 | bytes 1536 | tf_op jit(solution)/shard_map/neg | solution.py:240
  0.7 0.7 %convert_multiply_fusion = f32[3,256]{1,0:T(4,128)S(1)} fusion(bf16[3,256]{1,0:T(4,128)(2,1)} %param.5, f32[256]{0:T(256)S(1)} %exponential-minus-one_negate_fusion), kind=kLoop, calls=%fused_computation.1 | loop fusion | flops 1536 | bytes 5632 | tf_op jit(solution)/shard_map/mul | solution.py:241
  1.4 0.6 %reshape.14.table_ref = f32[8,128]{1,0:T(8,128)} reshape(f32[4,256]{1,0:T(4,128)S(1)} %pad_maximum_fusion) | data formatting | bytes 8192 | tf_op jit(solution)/shard_map/reshape | solution.py:242
  2.0 27.8 %render_exchange.1 = f32[16,8,256]{2,1,0:T(8,128)} custom-call(s32[8,16,2,8,256]{4,3,2,1,0:T(8,128)} %bitcast.6, f32[8,128]{1,0:T(8,128)} %reshape.14.table_ref, s32[8,16]{1,0:T(8,128)} %bitcast.8), custom_call_target="tpu_custom_call" | custom-call | tf_op jit(solution)/shard_map/render_exchange/pallas_call | solution.py:245
  29.8 1.0 %reshape.15 = f32[16,4,2,256]{3,2,1,0:T(2,128)S(1)} reshape(f32[16,8,256]{2,1,0:T(8,128)} %render_exchange.1) | data formatting | bytes 262144 | tf_op jit(solution)/shard_map/reshape | solution.py:275
  30.8 0.7 %copy.6 = f32[16,4,1,2,256]{4,3,0,2,1:T(2,128)} copy(f32[16,4,1,2,256]{4,3,2,1,0:T(2,128)S(1)} %bitcast.7) | data formatting | bytes 262144 | tf_op jit(solution)/shard_map/reshape | solution.py:276
  (1 shorter events, 0.0 us)

commit v2 on v1

v2 whole, which is shorter than its diff:
```python
import jax
import jax.numpy as jnp
from jax import lax
from jax.experimental import pallas as pl
from jax.experimental.pallas import tpu as pltpu
from jax.sharding import PartitionSpec as P

extinction = 3.0
MESH = pl.DeviceIdType.MESH


def ring(step):
    return min(step, 4 - step)


OFFSETS = sorted(
    [(dx, dz) for dx in range(4) for dz in range(4)],
    key=lambda o: (-(ring(o[0]) + ring(o[1])), (o[0] * 5 + o[1] * 3) % 11),
)
PEERS = len(OFFSETS) - 1
NEAR = [(2, 0), (2, 1), (3, 0), (3, 1), (1, 0), (1, 1), (0, 1), (0, 0)]
SLOTS = len(NEAR) - 1


def coords():
    depth = lax.axis_index("depth")
    screen = lax.axis_index("screen")
    return depth // 2, (depth % 2) * 2 + screen // 8, (screen // 2) % 4, screen % 2


def device(x, z, y, core):
    return {"depth": x * 2 + z // 2, "screen": (z % 2) * 8 + y * 2 + core}


def gather_lanes(table, lanes):
    numbers = lax.GatherDimensionNumbers(
        offset_dims=(),
        collapsed_slice_dims=(1,),
        start_index_map=(1,),
        operand_batching_dims=(0,),
        start_indices_batching_dims=(0,),
    )
    return lax.gather(
        table, lanes[..., None], numbers, slice_sizes=(1, 1), mode=lax.GatherScatterMode.PROMISE_IN_BOUNDS
    )


def shade(patches, tables):
    sums = [None] * len(patches)
    for j in range(len(patches[0])):
        for i, bins in enumerate(patches):
            lanes = bins[j] & 127
            low = bins[j] < 128
            values = [
                jnp.where(low, gather_lanes(tables[2 * ch], lanes), gather_lanes(tables[2 * ch + 1], lanes))
                for ch in range(4)
            ]
            if j == 0:
                sums[i] = values
            else:
                clear = 1.0 - sums[i][3]
                sums[i] = [s + clear * v for s, v in zip(sums[i], values)]
    return sums


def regroup(planes, pair):
    low_half = pair < 2
    even = (pair % 2) == 0
    u0 = jnp.where(low_half, planes[0], pltpu.roll(planes[2], 4, 0))
    u1 = jnp.where(low_half, planes[1], pltpu.roll(planes[3], 4, 0))
    v0 = jnp.where(low_half, pltpu.roll(planes[0], 4, 0), planes[2])
    v1 = jnp.where(low_half, pltpu.roll(planes[1], 4, 0), planes[3])
    return [
        jnp.where(even, u0, pltpu.roll(u1, 2, 0)),
        jnp.where(even, pltpu.roll(u0, 6, 0), u1),
        jnp.where(even, v0, pltpu.roll(v1, 2, 0)),
        jnp.where(even, pltpu.roll(v0, 6, 0), v1),
    ]


def kernel(
    vox, colors, opacity, order, out_ref,
    vin, colors_in, opacity_in, order_in, send_far, send_near, recv_far, recv_sib, recv_other, recv_own, result, landed,
    place, small_sem, load_sem, self_sem, send_sem, recv_sem, send2_sem, recv2_sem,
):
    x, z, y, core = coords()
    half = y // 2
    slab = x * 2 + z // 2
    side = z % 2
    sibling = y + 1 - 2 * (y % 2)
    ys = [y, sibling, (y + 2) % 4, (sibling + 2) % 4]
    cores = [core, 1 - core]

    def load(part):
        source = half if part else 1 - half
        return pltpu.make_async_copy(vox.at[:, :, source], vin.at[part], load_sem.at[part])

    small = [
        pltpu.make_async_copy(colors, colors_in, small_sem.at[0]),
        pltpu.make_async_copy(opacity, opacity_in, small_sem.at[1]),
        pltpu.make_async_copy(order, order_in, small_sem.at[2]),
    ]
    for copy in small[:2]:
        copy.start()
    load(0).start()
    load(1).start()
    small[2].start()

    barrier = pltpu.get_barrier_semaphore()
    for dx, dz in OFFSETS[:-1]:
        pl.semaphore_signal(
            barrier, inc=1, device_id=device((x + dx) % 4, (z + dz) % 4, y, core), device_id_type=MESH
        )
    for yrel, crel in NEAR[:-1]:
        pl.semaphore_signal(barrier, inc=1, device_id=device(x, z, ys[yrel], cores[crel]), device_id_type=MESH)

    small[0].wait()
    small[1].wait()
    alpha = 1.0 - jnp.exp(-(extinction / 64) * opacity_in[...].astype(jnp.float32).reshape(1, 256))
    shaded = colors_in[...].astype(jnp.float32) * alpha
    tables = [
        jnp.broadcast_to((shaded[ch : ch + 1] if ch < 3 else alpha)[:, part * 128 : part * 128 + 128], (8, 128))
        for ch in range(4)
        for part in range(2)
    ]
    pair = lax.broadcasted_iota(jnp.int32, (8, 128), 0) // 2

    def place_of(k):
        dx, dz = OFFSETS[k]
        return (x + dx) % 4, (z + dz) % 4

    def render(part, ks):
        blocks = [to_x * 4 + to_z for to_x, to_z in map(place_of, ks)]
        spots = [(b, pl.ds(col * 128, 128)) for b in blocks for col in range(2)]
        for (b, span), planes in zip(
            spots, shade([[vin[part, j, b, :, span] for j in range(8)] for b, span in spots], tables)
        ):
            for q, rows in enumerate(regroup(planes, pair)):
                if part == 0:
                    send_far[b, q // 2, q % 2, :, span] = rows
                else:
                    send_near[(q // 2 + y) % 2, b, q % 2, :, span] = rows

    buffers = [
        (lambda b: send_far.at[b], recv_far),
        (lambda b: send_near.at[1, b], recv_sib),
        (lambda b: send_near.at[0, b, 1 - core], recv_other),
        (lambda b: send_near.at[0, b, core], recv_own),
    ]

    def message(group, k):
        to_x, to_z = place_of(k)
        source, target = buffers[group]
        return pltpu.make_async_remote_copy(
            src_ref=source(to_x * 4 + to_z),
            dst_ref=target.at[side, slab],
            send_sem=send_sem.at[group, k],
            recv_sem=recv_sem.at[group, k],
            device_id=device(to_x, to_z, y, core),
            device_id_type=MESH,
        )

    def keep(group):
        source, target = buffers[group]
        return pltpu.make_async_copy(source(x * 4 + z), target.at[side, slab], self_sem.at[group])

    def send(group, k):
        if k < PEERS:
            message(group, k).start()
        else:
            keep(group).start()

    def arrive(group):
        for k in range(PEERS):
            message(group, k).wait_recv()
        keep(group).wait()

    load(0).wait()
    for k in range(0, PEERS + 1, 2):
        render(0, [k, k + 1])
        if k == 0:
            pl.semaphore_wait(barrier, PEERS + SLOTS)
        send(0, k)
        send(0, k + 1)
    load(1).wait()
    for k in range(0, PEERS + 1, 2):
        render(1, [k, k + 1])
        send(1, k)
        send(1, k + 1)
    for group in (2, 3):
        for k in range(PEERS + 1):
            send(group, k)

    small[2].wait()
    for t in range(2):
        row = t * 8 + y * 2 + core
        places = [order_in[i, row] for i in range(8)]
        for k in range(8):
            found = jnp.int32(0)
            for i in range(8):
                found = jnp.where(places[i] == k, jnp.int32(i), found)
            place[t * 8 + k] = found

    alpha_rows = 6 + lax.broadcasted_iota(jnp.int32, (8, 128), 0) % 2

    def over(read, store):
        for t in range(2):
            for col in range(2):
                span = pl.ds(col * 128, 128)
                total = read(t, place[t * 8], span)
                for k in range(1, 8):
                    alpha = jnp.take_along_axis(total, alpha_rows, axis=0, mode="promise_in_bounds")
                    total = total + (1.0 - alpha) * read(t, place[t * 8 + k], span)
                store(t, span, total)

    def forward(slot):
        yrel, crel = NEAR[slot]
        return pltpu.make_async_remote_copy(
            src_ref=result.at[yrel, cores[crel]],
            dst_ref=landed.at[yrel, core],
            send_sem=send2_sem.at[slot],
            recv_sem=recv2_sem.at[slot],
            device_id=device(x, z, ys[yrel], cores[crel]),
            device_id_type=MESH,
        )

    def pass_on(slot, read):
        yrel, crel = NEAR[slot]

        def store(t, span, total):
            result[yrel, cores[crel], t, :, span] = total

        over(read, store)
        if slot < SLOTS:
            forward(slot).start()

    def put(yrel):
        for t in range(2):
            blocks = [landed[yrel, c, t, :, pl.ds(col * 128, 128)] for c in range(2) for col in range(2)]
            for ch, rows in enumerate(regroup(blocks, pair)):
                out_ref[ch * 8 + t * 4 + ys[yrel]] = rows

    arrive(0)
    for slot in range(4):
        yrel, crel = NEAR[slot]
        pass_on(slot, lambda t, s, span: recv_far[t, s, ys[yrel] % 2, cores[crel], :, span])
    arrive(1)
    for slot in range(4, 6):
        crel = NEAR[slot][1]
        pass_on(slot, lambda t, s, span: recv_sib[t, s, cores[crel], :, span])
    arrive(2)
    pass_on(6, lambda t, s, span: recv_other[t, s, :, span])
    for slot in range(4):
        forward(slot).wait_recv()
    put(2)
    put(3)
    arrive(3)

    def store_own(t, span, total):
        landed[0, core, t, :, span] = total

    over(lambda t, s, span: recv_own[t, s, :, span], store_own)
    for slot in range(4, SLOTS):
        forward(slot).wait_recv()
    put(1)
    put(0)

    for group in range(4):
        for k in range(PEERS):
            message(group, k).wait_send()
    for slot in range(SLOTS):
        forward(slot).wait_send()


def local(voxel_bins, colors, opacity, slab_order):
    f32 = jnp.float32
    out = pl.pallas_call(
        kernel,
        out_shape=jax.ShapeDtypeStruct((32, 8, 128), f32),
        in_specs=[pl.BlockSpec(memory_space=pl.ANY)] * 4,
        out_specs=pl.BlockSpec(memory_space=pltpu.VMEM),
        scratch_shapes=[
            pltpu.VMEM((2, 8, 16, 8, 256), jnp.int32),
            pltpu.VMEM((3, 256), jnp.bfloat16),
            pltpu.VMEM((256,), jnp.bfloat16),
            pltpu.SMEM((8, 16), jnp.int32),
            pltpu.VMEM((16, 2, 2, 8, 256), f32),
            pltpu.VMEM((2, 16, 2, 8, 256), f32),
            pltpu.VMEM((2, 8, 2, 2, 8, 256), f32),
            pltpu.VMEM((2, 8, 2, 8, 256), f32),
            pltpu.VMEM((2, 8, 8, 256), f32),
            pltpu.VMEM((2, 8, 8, 256), f32),
            pltpu.VMEM((4, 2, 2, 8, 256), f32),
            pltpu.VMEM((4, 2, 2, 8, 256), f32),
            pltpu.SMEM((16,), jnp.int32),
            pltpu.SemaphoreType.DMA((3,)),
            pltpu.SemaphoreType.DMA((2,)),
            pltpu.SemaphoreType.DMA((4,)),
            pltpu.SemaphoreType.DMA((4, PEERS)),
            pltpu.SemaphoreType.DMA((4, PEERS)),
            pltpu.SemaphoreType.DMA((SLOTS,)),
            pltpu.SemaphoreType.DMA((SLOTS,)),
        ],
        compiler_params=pltpu.CompilerParams(collective_id=0, has_side_effects=True),
        name="render_exchange",
    )(voxel_bins.reshape(8, 16, 2, 8, 256), colors, opacity, slab_order.T)
    return jnp.transpose(out.reshape(4, 32, 2, 128), (0, 2, 1, 3)).reshape(4, 2, 4096)


def solution(mesh):
    placed = (P("depth", None, "screen"), P(), P(), P())
    return jax.shard_map(
        local,
        mesh=mesh,
        in_specs=placed,
        out_specs=P(None, ("depth", "screen"), None),
        check_vma=False,
    )
```

time: 31.7 us -> 28 us (0.88)
  Pallas kernels: 27.8 us -> 26.3 us
  other arithmetic: 1.36 us -> 0 us
  local copies, waits for them, and re-layouts: 2.26 us -> 1.57 us
    reshape x3 -> x0, local copies, waits for them, and re-layouts: 2.26 us -> none  [the longest x1 0.98 us: local(): out = out.reshape(16, 4, 2, 256)]
    unnamed x0 -> x1, local copies, waits for them, and re-layouts: none -> 1.57 us
    pallas_call x1, Pallas kernels: 27.8 us -> 26.3 us  [local(): pl.pallas_call(kernel, out_shape=jax.ShapeDtypeStruct((32, 8, 128), f32),...]
    mul x1 -> x0, other arithmetic: 0.69 us -> none  [local(): colors.astype(jnp.float32) * alpha[None]]
    neg x1 -> x0, other arithmetic: 0.66 us -> none  [local(): alpha = -jnp.expm1(-rate * opacity.astype(jnp.float32))]
where the time goes in v2:
time: 28 us; the launch traced here: 27.9 us
  Pallas kernels  26.3 us (94%)
  local copies, waits for them, and re-layouts  1.57 us (6%)
    pallas_call x1, Pallas kernels, local(): pl.pallas_call(kernel, out_shape=jax.ShapeDtypeStruct((32, 8, 128), f32),...  26.3 us
    unnamed x1, local copies, waits for them, and re-layouts  1.57 us

profile of v2, /device:TPU:1, one launch (start us, length us, event | category | flops | bytes accessed | tf_op | source)
XLA Modules:
  0.0 27.9 jit_solution(6532036767275362305)
XLA Ops:
  0.0 26.3 %render_exchange.1 = f32[32,8,128]{2,1,0:T(8,128)} custom-call(s32[8,16,2,8,256]{4,3,2,1,0:T(8,128)} %bitcast.7, bf16[3,256]{1,0:T(4,128)(2,1)} %colors.1, bf16[256]{0:T(256)(128)(2,1)} %opacity.1, s32[8,16]{1,0:T(8,128)} %bitcast.9), custom_call_target="tpu_custom_call" | custom-call | tf_op jit(solution)/shard_map/render_exchange/pallas_call | solution.py:277
  26.3 1.6 %copy.7 = f32[4,2,4096]{2,1,0:T(2,128)} copy(f32[4,2,4096]{2,1,0:T(2,128)} %bitcast.8) | data formatting | bytes 262144

commit v3 on v2

--- a/solution.py
+++ b/solution.py
@@ -15,7 +15,7 @@
 
 OFFSETS = sorted(
     [(dx, dz) for dx in range(4) for dz in range(4)],
-    key=lambda o: (-(ring(o[0]) + ring(o[1])), (o[0] * 5 + o[1] * 3) % 11),
+    key=lambda o: (o == (0, 0), (o[0] * 5 + o[1] * 3) % 11),
 )
 PEERS = len(OFFSETS) - 1
 NEAR = [(2, 0), (2, 1), (3, 0), (3, 1), (1, 0), (1, 1), (0, 1), (0, 0)]
@@ -81,7 +81,7 @@
 def kernel(
     vox, colors, opacity, order, out_ref,
     vin, colors_in, opacity_in, order_in, send_far, send_near, recv_far, recv_sib, recv_other, recv_own, result, landed,
-    place, small_sem, load_sem, self_sem, send_sem, recv_sem, send2_sem, recv2_sem,
+    place, small_sem, load_sem, send_sem, recv_sem, send2_sem, recv2_sem,
 ):
     x, z, y, core = coords()
     half = y // 2
@@ -154,15 +154,15 @@
         return pltpu.make_async_remote_copy(
             src_ref=source(to_x * 4 + to_z),
             dst_ref=target.at[side, slab],
-            send_sem=send_sem.at[group, k],
-            recv_sem=recv_sem.at[group, k],
+            send_sem=send_sem.at[min(group, 2)],
+            recv_sem=recv_sem.at[group],
             device_id=device(to_x, to_z, y, core),
             device_id_type=MESH,
         )
 
     def keep(group):
         source, target = buffers[group]
-        return pltpu.make_async_copy(source(x * 4 + z), target.at[side, slab], self_sem.at[group])
+        return pltpu.make_async_copy(source(x * 4 + z), target.at[side, slab], recv_sem.at[group])
 
     def send(group, k):
         if k < PEERS:
@@ -171,9 +171,8 @@
             keep(group).start()
 
     def arrive(group):
-        for k in range(PEERS):
-            message(group, k).wait_recv()
-        keep(group).wait()
+        whole = buffers[group][1]
+        pltpu.make_async_copy(whole, whole, recv_sem.at[group]).wait()
 
     load(0).wait()
     for k in range(0, PEERS + 1, 2):
@@ -216,27 +215,28 @@
     def forward(slot):
         yrel, crel = NEAR[slot]
         return pltpu.make_async_remote_copy(
-            src_ref=result.at[yrel, cores[crel]],
-            dst_ref=landed.at[yrel, core],
-            send_sem=send2_sem.at[slot],
-            recv_sem=recv2_sem.at[slot],
+            src_ref=result.at[slot],
+            dst_ref=landed.at[yrel * 2 + core],
+            send_sem=send2_sem.at[0],
+            recv_sem=recv2_sem.at[slot // 4 + slot // 6],
             device_id=device(x, z, ys[yrel], cores[crel]),
             device_id_type=MESH,
         )
 
     def pass_on(slot, read):
-        yrel, crel = NEAR[slot]
-
         def store(t, span, total):
-            result[yrel, cores[crel], t, :, span] = total
+            result[slot, t, :, span] = total
 
         over(read, store)
-        if slot < SLOTS:
-            forward(slot).start()
+        forward(slot).start()
+
+    def land(group):
+        part = landed.at[(pl.ds(4, 4), pl.ds(2, 2), pl.ds(0, 1))[group]]
+        pltpu.make_async_copy(part, part, recv2_sem.at[group]).wait()
 
     def put(yrel):
         for t in range(2):
-            blocks = [landed[yrel, c, t, :, pl.ds(col * 128, 128)] for c in range(2) for col in range(2)]
+            blocks = [landed[yrel * 2 + c, t, :, pl.ds(col * 128, 128)] for c in range(2) for col in range(2)]
             for ch, rows in enumerate(regroup(blocks, pair)):
                 out_ref[ch * 8 + t * 4 + ys[yrel]] = rows
 
@@ -250,33 +250,32 @@
         pass_on(slot, lambda t, s, span: recv_sib[t, s, cores[crel], :, span])
     arrive(2)
     pass_on(6, lambda t, s, span: recv_other[t, s, :, span])
-    for slot in range(4):
-        forward(slot).wait_recv()
+    land(0)
     put(2)
     put(3)
     arrive(3)
 
     def store_own(t, span, total):
-        landed[0, core, t, :, span] = total
+        landed[core, t, :, span] = total
 
     over(lambda t, s, span: recv_own[t, s, :, span], store_own)
-    for slot in range(4, SLOTS):
-        forward(slot).wait_recv()
+    land(1)
     put(1)
+    land(2)
     put(0)
 
-    for group in range(4):
-        for k in range(PEERS):
-            message(group, k).wait_send()
-    for slot in range(SLOTS):
-        forward(slot).wait_send()
+    sent = [send_far.at[pl.ds(0, PEERS)], send_near.at[1, pl.ds(0, PEERS)], send_near.at[0, pl.ds(0, PEERS)]]
+    for group, part in enumerate(sent):
+        pltpu.make_async_copy(part, part, send_sem.at[group]).wait()
+    part = result.at[pl.ds(0, SLOTS)]
+    pltpu.make_async_copy(part, part, send2_sem.at[0]).wait()
 
 
 def local(voxel_bins, colors, opacity, slab_order):
     f32 = jnp.float32
     out = pl.pallas_call(
         kernel,
-        out_shape=jax.ShapeDtypeStruct((32, 8, 128), f32),
+        out_shape=pltpu.VMEM((32, 8, 128), f32),
         in_specs=[pl.BlockSpec(memory_space=pl.ANY)] * 4,
         out_specs=pl.BlockSpec(memory_space=pltpu.VMEM),
         scratch_shapes=[
@@ -290,16 +289,15 @@
             pltpu.VMEM((2, 8, 2, 8, 256), f32),
             pltpu.VMEM((2, 8, 8, 256), f32),
             pltpu.VMEM((2, 8, 8, 256), f32),
-            pltpu.VMEM((4, 2, 2, 8, 256), f32),
-            pltpu.VMEM((4, 2, 2, 8, 256), f32),
+            pltpu.VMEM((8, 2, 8, 256), f32),
+            pltpu.VMEM((8, 2, 8, 256), f32),
             pltpu.SMEM((16,), jnp.int32),
             pltpu.SemaphoreType.DMA((3,)),
             pltpu.SemaphoreType.DMA((2,)),
+            pltpu.SemaphoreType.DMA((3,)),
             pltpu.SemaphoreType.DMA((4,)),
-            pltpu.SemaphoreType.DMA((4, PEERS)),
-            pltpu.SemaphoreType.DMA((4, PEERS)),
-            pltpu.SemaphoreType.DMA((SLOTS,)),
-            pltpu.SemaphoreType.DMA((SLOTS,)),
+            pltpu.SemaphoreType.DMA((1,)),
+            pltpu.SemaphoreType.DMA((3,)),
         ],
         compiler_params=pltpu.CompilerParams(collective_id=0, has_side_effects=True),
         name="render_exchange",

time: 28 us -> 23.9 us (0.85)
  Pallas kernels: 26.3 us -> 23.1 us
  local copies, waits for them, and re-layouts: 1.57 us -> 0.66 us
    pallas_call x1, Pallas kernels: 26.3 us -> 23.1 us  [local(): pl.pallas_call(kernel, out_shape=pltpu.VMEM((32, 8, 128), f32), in_specs=...]
    unnamed x1, local copies, waits for them, and re-layouts: 1.57 us -> 0.66 us
where the time goes in v3:
time: 23.9 us; the launch traced here: 23.7 us
  Pallas kernels  23.1 us (97%)
  local copies, waits for them, and re-layouts  0.66 us (3%)
    pallas_call x1, Pallas kernels, local(): pl.pallas_call(kernel, out_shape=pltpu.VMEM((32, 8, 128), f32), in_specs=...  23.1 us
    unnamed x1, local copies, waits for them, and re-layouts  0.66 us

profile of v3, /device:TPU:1, one launch (start us, length us, event | category | flops | bytes accessed | tf_op | source)
XLA Modules:
  0.0 23.7 jit_solution(4589189493702622551)
XLA Ops:
  0.0 23.1 %render_exchange.1 = f32[32,8,128]{2,1,0:T(8,128)S(1)} custom-call(s32[8,16,2,8,256]{4,3,2,1,0:T(8,128)} %bitcast.8, bf16[3,256]{1,0:T(4,128)(2,1)} %colors.1, bf16[256]{0:T(256)(128)(2,1)} %opacity.1, s32[8,16]{1,0:T(8,128)} %bitcast.9), custom_call_target="tpu_custom_call" | custom-call | tf_op jit(solution)/shard_map/render_exchange/pallas_call | solution.py:276
  23.1 0.7 %copy.7 = f32[4,2,4096]{2,1,0:T(2,128)} copy(f32[4,2,4096]{2,1,0:T(2,128)S(1)} %bitcast.7) | data formatting | bytes 262144

commit v4 on v3

--- a/solution.py
+++ b/solution.py
@@ -20,6 +20,7 @@
 PEERS = len(OFFSETS) - 1
 NEAR = [(2, 0), (2, 1), (3, 0), (3, 1), (1, 0), (1, 1), (0, 1), (0, 0)]
 SLOTS = len(NEAR) - 1
+GROUPS = [(0, 1, 2, 3), (4, 5), (6,), (7,)]
 
 
 def coords():
@@ -80,8 +81,8 @@
 
 def kernel(
     vox, colors, opacity, order, out_ref,
-    vin, colors_in, opacity_in, order_in, send_far, send_near, recv_far, recv_sib, recv_other, recv_own, result, landed,
-    place, small_sem, load_sem, send_sem, recv_sem, send2_sem, recv2_sem,
+    vin, colors_in, opacity_in, order_in, packed, result, landed, place, small_sem, load_sem, send_sem, recv_sem,
+    send2_sem, recv2_sem, *received
 ):
     x, z, y, core = coords()
     half = y // 2
@@ -90,6 +91,14 @@
     sibling = y + 1 - 2 * (y % 2)
     ys = [y, sibling, (y + 2) % 4, (sibling + 2) % 4]
     cores = [core, 1 - core]
+
+    barrier = pltpu.get_barrier_semaphore()
+    for dx, dz in sorted(OFFSETS[:-1], key=lambda o: -(ring(o[0]) + ring(o[1]))):
+        pl.semaphore_signal(
+            barrier, inc=1, device_id=device((x + dx) % 4, (z + dz) % 4, y, core), device_id_type=MESH
+        )
+    for yrel, crel in NEAR[:-1]:
+        pl.semaphore_signal(barrier, inc=1, device_id=device(x, z, ys[yrel], cores[crel]), device_id_type=MESH)
 
     def load(part):
         source = half if part else 1 - half
@@ -106,14 +115,6 @@
     load(1).start()
     small[2].start()
 
-    barrier = pltpu.get_barrier_semaphore()
-    for dx, dz in OFFSETS[:-1]:
-        pl.semaphore_signal(
-            barrier, inc=1, device_id=device((x + dx) % 4, (z + dz) % 4, y, core), device_id_type=MESH
-        )
-    for yrel, crel in NEAR[:-1]:
-        pl.semaphore_signal(barrier, inc=1, device_id=device(x, z, ys[yrel], cores[crel]), device_id_type=MESH)
-
     small[0].wait()
     small[1].wait()
     alpha = 1.0 - jnp.exp(-(extinction / 64) * opacity_in[...].astype(jnp.float32).reshape(1, 256))
@@ -136,33 +137,29 @@
             spots, shade([[vin[part, j, b, :, span] for j in range(8)] for b, span in spots], tables)
         ):
             for q, rows in enumerate(regroup(planes, pair)):
-                if part == 0:
-                    send_far[b, q // 2, q % 2, :, span] = rows
-                else:
-                    send_near[(q // 2 + y) % 2, b, q % 2, :, span] = rows
-
-    buffers = [
-        (lambda b: send_far.at[b], recv_far),
-        (lambda b: send_near.at[1, b], recv_sib),
-        (lambda b: send_near.at[0, b, 1 - core], recv_other),
-        (lambda b: send_near.at[0, b, core], recv_own),
-    ]
+                rel, crel = (q // 2 + y) % 2, (q + core) % 2
+                slot = rel * (4 + crel) + (1 - rel) * (7 - crel) if part else rel * 2 + crel
+                packed[b, slot, :, span] = rows
+
+    def ends(group, b):
+        slots = GROUPS[group]
+        return packed.at[b, pl.ds(slots[0], len(slots))], received[group].at[side, slab]
 
     def message(group, k):
         to_x, to_z = place_of(k)
-        source, target = buffers[group]
+        source, target = ends(group, to_x * 4 + to_z)
         return pltpu.make_async_remote_copy(
-            src_ref=source(to_x * 4 + to_z),
-            dst_ref=target.at[side, slab],
-            send_sem=send_sem.at[min(group, 2)],
+            src_ref=source,
+            dst_ref=target,
+            send_sem=send_sem.at[0],
             recv_sem=recv_sem.at[group],
             device_id=device(to_x, to_z, y, core),
             device_id_type=MESH,
         )
 
     def keep(group):
-        source, target = buffers[group]
-        return pltpu.make_async_copy(source(x * 4 + z), target.at[side, slab], recv_sem.at[group])
+        source, target = ends(group, x * 4 + z)
+        return pltpu.make_async_copy(source, target, recv_sem.at[group])
 
     def send(group, k):
         if k < PEERS:
@@ -171,24 +168,22 @@
             keep(group).start()
 
     def arrive(group):
-        whole = buffers[group][1]
+        whole = received[group]
         pltpu.make_async_copy(whole, whole, recv_sem.at[group]).wait()
 
-    load(0).wait()
-    for k in range(0, PEERS + 1, 2):
-        render(0, [k, k + 1])
-        if k == 0:
-            pl.semaphore_wait(barrier, PEERS + SLOTS)
-        send(0, k)
-        send(0, k + 1)
-    load(1).wait()
-    for k in range(0, PEERS + 1, 2):
-        render(1, [k, k + 1])
-        send(1, k)
-        send(1, k + 1)
-    for group in (2, 3):
-        for k in range(PEERS + 1):
-            send(group, k)
+    for part in range(2):
+        load(part).wait()
+        mine = [g for g, slots in enumerate(GROUPS) if (slots[-1] > 3) == bool(part)]
+        for k in range(0, PEERS + 1, 2):
+            render(part, [k, k + 1])
+            if part == 0 and k == 0:
+                pl.semaphore_wait(barrier, PEERS + SLOTS)
+            for group in mine[:1]:
+                send(group, k)
+                send(group, k + 1)
+        for group in mine[1:]:
+            for k in range(PEERS + 1):
+                send(group, k)
 
     small[2].wait()
     for t in range(2):
@@ -240,33 +235,27 @@
             for ch, rows in enumerate(regroup(blocks, pair)):
                 out_ref[ch * 8 + t * 4 + ys[yrel]] = rows
 
-    arrive(0)
-    for slot in range(4):
-        yrel, crel = NEAR[slot]
-        pass_on(slot, lambda t, s, span: recv_far[t, s, ys[yrel] % 2, cores[crel], :, span])
-    arrive(1)
-    for slot in range(4, 6):
-        crel = NEAR[slot][1]
-        pass_on(slot, lambda t, s, span: recv_sib[t, s, cores[crel], :, span])
-    arrive(2)
-    pass_on(6, lambda t, s, span: recv_other[t, s, :, span])
-    land(0)
-    put(2)
-    put(3)
-    arrive(3)
-
     def store_own(t, span, total):
         landed[core, t, :, span] = total
 
-    over(lambda t, s, span: recv_own[t, s, :, span], store_own)
+    for group, slots in enumerate(GROUPS):
+        arrive(group)
+        for i, slot in enumerate(slots):
+            read = lambda t, s, span: received[group][t, s, i, :, span]
+            if slot < SLOTS:
+                pass_on(slot, read)
+            else:
+                land(0)
+                put(2)
+                put(3)
+                over(read, store_own)
     land(1)
     put(1)
     land(2)
     put(0)
 
-    sent = [send_far.at[pl.ds(0, PEERS)], send_near.at[1, pl.ds(0, PEERS)], send_near.at[0, pl.ds(0, PEERS)]]
-    for group, part in enumerate(sent):
-        pltpu.make_async_copy(part, part, send_sem.at[group]).wait()
+    part = packed.at[pl.ds(0, PEERS)]
+    pltpu.make_async_copy(part, part, send_sem.at[0]).wait()
     part = result.at[pl.ds(0, SLOTS)]
     pltpu.make_async_copy(part, part, send2_sem.at[0]).wait()
 
@@ -283,21 +272,17 @@
             pltpu.VMEM((3, 256), jnp.bfloat16),
             pltpu.VMEM((256,), jnp.bfloat16),
             pltpu.SMEM((8, 16), jnp.int32),
-            pltpu.VMEM((16, 2, 2, 8, 256), f32),
-            pltpu.VMEM((2, 16, 2, 8, 256), f32),
-            pltpu.VMEM((2, 8, 2, 2, 8, 256), f32),
-            pltpu.VMEM((2, 8, 2, 8, 256), f32),
-            pltpu.VMEM((2, 8, 8, 256), f32),
-            pltpu.VMEM((2, 8, 8, 256), f32),
+            pltpu.VMEM((16, 8, 8, 256), f32),
             pltpu.VMEM((8, 2, 8, 256), f32),
             pltpu.VMEM((8, 2, 8, 256), f32),
             pltpu.SMEM((16,), jnp.int32),
             pltpu.SemaphoreType.DMA((3,)),
             pltpu.SemaphoreType.DMA((2,)),
-            pltpu.SemaphoreType.DMA((3,)),
-            pltpu.SemaphoreType.DMA((4,)),
+            pltpu.SemaphoreType.DMA((1,)),
+            pltpu.SemaphoreType.DMA((len(GROUPS),)),
             pltpu.SemaphoreType.DMA((1,)),
             pltpu.SemaphoreType.DMA((3,)),
+            *[pltpu.VMEM((2, 8, len(slots), 8, 256), f32) for slots in GROUPS],
         ],
         compiler_params=pltpu.CompilerParams(collective_id=0, has_side_effects=True),
         name="render_exchange",

time: 23.9 us -> 23.8 us (level)
  no operation moved by 1% of the time
where the time goes in v4:
time: 23.8 us; the launch traced here: 23.7 us
  Pallas kernels  23 us (97%)
  local copies, waits for them, and re-layouts  0.66 us (3%)
    pallas_call x1, Pallas kernels, local(): pl.pallas_call(kernel, out_shape=pltpu.VMEM((32, 8, 128), f32), in_specs=...  23 us
    unnamed x1, local copies, waits for them, and re-layouts  0.66 us

profile of v4, /device:TPU:1, one launch (start us, length us, event | category | flops | bytes accessed | tf_op | source)
XLA Modules:
  0.0 23.7 jit_solution(7180470136443128062)
XLA Ops:
  0.0 23.0 %render_exchange.1 = f32[32,8,128]{2,1,0:T(8,128)S(1)} custom-call(s32[8,16,2,8,256]{4,3,2,1,0:T(8,128)} %bitcast.8, bf16[3,256]{1,0:T(4,128)(2,1)} %colors.1, bf16[256]{0:T(256)(128)(2,1)} %opacity.1, s32[8,16]{1,0:T(8,128)} %bitcast.9), custom_call_target="tpu_custom_call" | custom-call | tf_op jit(solution)/shard_map/render_exchange/pallas_call | solution.py:265
  23.0 0.7 %copy.7 = f32[4,2,4096]{2,1,0:T(2,128)} copy(f32[4,2,4096]{2,1,0:T(2,128)S(1)} %bitcast.7) | data formatting | bytes 262144

commit v5 on v4

--- a/solution.py
+++ b/solution.py
@@ -26,11 +26,16 @@
 def coords():
     depth = lax.axis_index("depth")
     screen = lax.axis_index("screen")
-    return depth // 2, (depth % 2) * 2 + screen // 8, (screen // 2) % 4, screen % 2
+    return (
+        lax.div(depth, 2),
+        lax.rem(depth, 2) * 2 + lax.div(screen, 8),
+        lax.rem(lax.div(screen, 2), 4),
+        lax.rem(screen, 2),
+    )
 
 
 def device(x, z, y, core):
-    return {"depth": x * 2 + z // 2, "screen": (z % 2) * 8 + y * 2 + core}
+    return {"depth": x * 2 + lax.div(z, 2), "screen": lax.rem(z, 2) * 8 + y * 2 + core}
 
 
 def gather_lanes(table, lanes):
@@ -85,24 +90,38 @@
     send2_sem, recv2_sem, *received
 ):
     x, z, y, core = coords()
-    half = y // 2
-    slab = x * 2 + z // 2
-    side = z % 2
-    sibling = y + 1 - 2 * (y % 2)
-    ys = [y, sibling, (y + 2) % 4, (sibling + 2) % 4]
+    half = lax.div(y, 2)
+    slab = x * 2 + lax.div(z, 2)
+    side = lax.rem(z, 2)
+    sibling = y + 1 - 2 * lax.rem(y, 2)
+    ys = [y, sibling, lax.rem(y + 2, 4), lax.rem(sibling + 2, 4)]
     cores = [core, 1 - core]
 
     barrier = pltpu.get_barrier_semaphore()
     for dx, dz in sorted(OFFSETS[:-1], key=lambda o: -(ring(o[0]) + ring(o[1]))):
         pl.semaphore_signal(
-            barrier, inc=1, device_id=device((x + dx) % 4, (z + dz) % 4, y, core), device_id_type=MESH
+            barrier, inc=1, device_id=device(lax.rem(x + dx, 4), lax.rem(z + dz, 4), y, core), device_id_type=MESH
         )
     for yrel, crel in NEAR[:-1]:
         pl.semaphore_signal(barrier, inc=1, device_id=device(x, z, ys[yrel], cores[crel]), device_id_type=MESH)
 
-    def load(part):
-        source = half if part else 1 - half
-        return pltpu.make_async_copy(vox.at[:, :, source], vin.at[part], load_sem.at[part])
+    def place_of(k):
+        dx, dz = OFFSETS[k]
+        return lax.rem(x + dx, 4), lax.rem(z + dz, 4)
+
+    def block_of(k):
+        to_x, to_z = place_of(k)
+        return to_x * 4 + to_z
+
+    def load(k):
+        b = block_of(k)
+        return pltpu.make_async_copy(vox.at[:, b, 1 - half], vin.at[0, :, b], load_sem.at[min(k // 2, 1)])
+
+    def loaded(count, group):
+        part = vin.at[0, :, pl.ds(0, count)]
+        return pltpu.make_async_copy(part, part, load_sem.at[group])
+
+    load_own = pltpu.make_async_copy(vox.at[:, :, half], vin.at[1], load_sem.at[2])
 
     small = [
         pltpu.make_async_copy(colors, colors_in, small_sem.at[0]),
@@ -111,8 +130,9 @@
     ]
     for copy in small[:2]:
         copy.start()
-    load(0).start()
-    load(1).start()
+    for k in range(PEERS + 1):
+        load(k).start()
+    load_own.start()
     small[2].start()
 
     small[0].wait()
@@ -126,18 +146,14 @@
     ]
     pair = lax.broadcasted_iota(jnp.int32, (8, 128), 0) // 2
 
-    def place_of(k):
-        dx, dz = OFFSETS[k]
-        return (x + dx) % 4, (z + dz) % 4
-
     def render(part, ks):
-        blocks = [to_x * 4 + to_z for to_x, to_z in map(place_of, ks)]
+        blocks = [block_of(k) for k in ks]
         spots = [(b, pl.ds(col * 128, 128)) for b in blocks for col in range(2)]
         for (b, span), planes in zip(
             spots, shade([[vin[part, j, b, :, span] for j in range(8)] for b, span in spots], tables)
         ):
             for q, rows in enumerate(regroup(planes, pair)):
-                rel, crel = (q // 2 + y) % 2, (q + core) % 2
+                rel, crel = lax.rem(q // 2 + y, 2), lax.rem(q + core, 2)
                 slot = rel * (4 + crel) + (1 - rel) * (7 - crel) if part else rel * 2 + crel
                 packed[b, slot, :, span] = rows
 
@@ -172,15 +188,34 @@
         pltpu.make_async_copy(whole, whole, recv_sem.at[group]).wait()
 
     for part in range(2):
-        load(part).wait()
+        if part:
+            load_own.wait()
+        else:
+            loaded(2, 0).wait()
         mine = [g for g, slots in enumerate(GROUPS) if (slots[-1] > 3) == bool(part)]
         for k in range(0, PEERS + 1, 2):
+            if part == 0 and k == 2:
+                loaded(PEERS - 1, 1).wait()
             render(part, [k, k + 1])
             if part == 0 and k == 0:
                 pl.semaphore_wait(barrier, PEERS + SLOTS)
-            for group in mine[:1]:
-                send(group, k)
-                send(group, k + 1)
+            if part == 0:
+                send(0, k)
+                send(0, k + 1)
+                continue
+
+            @pl.when(core != 1)
+            def _():
+                send(1, k)
+                send(1, k + 1)
+
+        if part:
+
+            @pl.when(core == 1)
+            def _():
+                for k in range(PEERS + 1):
+                    send(1, k)
+
         for group in mine[1:]:
             for k in range(PEERS + 1):
                 send(group, k)
@@ -277,7 +312,7 @@
             pltpu.VMEM((8, 2, 8, 256), f32),
             pltpu.SMEM((16,), jnp.int32),
             pltpu.SemaphoreType.DMA((3,)),
-            pltpu.SemaphoreType.DMA((2,)),
+            pltpu.SemaphoreType.DMA((3,)),
             pltpu.SemaphoreType.DMA((1,)),
             pltpu.SemaphoreType.DMA((len(GROUPS),)),
             pltpu.SemaphoreType.DMA((1,)),

time: 23.8 us -> 23.6 us (level)
  no operation moved by 1% of the time
where the time goes in v5:
time: 23.6 us; the launch traced here: 23.5 us
  Pallas kernels  22.8 us (97%)
  local copies, waits for them, and re-layouts  0.66 us (3%)
    pallas_call x1, Pallas kernels, local(): pl.pallas_call(kernel, out_shape=pltpu.VMEM((32, 8, 128), f32), in_specs=...  22.8 us
    unnamed x1, local copies, waits for them, and re-layouts  0.66 us

profile of v5, /device:TPU:1, one launch (start us, length us, event | category | flops | bytes accessed | tf_op | source)
XLA Modules:
  0.0 23.5 jit_solution(15886773438365834416)
XLA Ops:
  0.0 22.8 %render_exchange.1 = f32[32,8,128]{2,1,0:T(8,128)S(1)} custom-call(s32[8,16,2,8,256]{4,3,2,1,0:T(8,128)} %bitcast.8, bf16[3,256]{1,0:T(4,128)(2,1)} %colors.1, bf16[256]{0:T(256)(128)(2,1)} %opacity.1, s32[8,16]{1,0:T(8,128)} %bitcast.9), custom_call_target="tpu_custom_call" | custom-call | tf_op jit(solution)/shard_map/render_exchange/pallas_call | solution.py:300
  22.8 0.7 %copy.7 = f32[4,2,4096]{2,1,0:T(2,128)} copy(f32[4,2,4096]{2,1,0:T(2,128)S(1)} %bitcast.7) | data formatting | bytes 262144

commit v6 on v5

--- a/solution.py
+++ b/solution.py
@@ -275,7 +275,7 @@
 
     for group, slots in enumerate(GROUPS):
         arrive(group)
-        for i, slot in enumerate(slots):
+        for i, slot in reversed(list(enumerate(slots))):
             read = lambda t, s, span: received[group][t, s, i, :, span]
             if slot < SLOTS:
                 pass_on(slot, read)

time: 23.6 us -> 23.6 us (level)
  no operation moved by 1% of the time
where the time goes in v6:
time: 23.6 us; the launch traced here: 23.5 us
  Pallas kernels  22.8 us (97%)
  local copies, waits for them, and re-layouts  0.66 us (3%)
    pallas_call x1, Pallas kernels, local(): pl.pallas_call(kernel, out_shape=pltpu.VMEM((32, 8, 128), f32), in_specs=...  22.8 us
    unnamed x1, local copies, waits for them, and re-layouts  0.66 us

profile of v6, /device:TPU:1, one launch (start us, length us, event | category | flops | bytes accessed | tf_op | source)
XLA Modules:
  0.0 23.5 jit_solution(4103339880205123513)
XLA Ops:
  0.0 22.8 %render_exchange.1 = f32[32,8,128]{2,1,0:T(8,128)S(1)} custom-call(s32[8,16,2,8,256]{4,3,2,1,0:T(8,128)} %bitcast.8, bf16[3,256]{1,0:T(4,128)(2,1)} %colors.1, bf16[256]{0:T(256)(128)(2,1)} %opacity.1, s32[8,16]{1,0:T(8,128)} %bitcast.9), custom_call_target="tpu_custom_call" | custom-call | tf_op jit(solution)/shard_map/render_exchange/pallas_call | solution.py:300
  22.8 0.7 %copy.7 = f32[4,2,4096]{2,1,0:T(2,128)} copy(f32[4,2,4096]{2,1,0:T(2,128)S(1)} %bitcast.7) | data formatting | bytes 262144

commit v7 on v6

--- a/solution.py
+++ b/solution.py
@@ -284,10 +284,10 @@
                 put(2)
                 put(3)
                 over(read, store_own)
+    land(2)
+    put(0)
     land(1)
     put(1)
-    land(2)
-    put(0)
 
     part = packed.at[pl.ds(0, PEERS)]
     pltpu.make_async_copy(part, part, send_sem.at[0]).wait()

time: 23.6 us -> 23.6 us (level)
  no operation moved by 1% of the time
where the time goes in v7:
time: 23.6 us; the launch traced here: 23.5 us
  Pallas kernels  22.8 us (97%)
  local copies, waits for them, and re-layouts  0.66 us (3%)
    pallas_call x1, Pallas kernels, local(): pl.pallas_call(kernel, out_shape=pltpu.VMEM((32, 8, 128), f32), in_specs=...  22.8 us
    unnamed x1, local copies, waits for them, and re-layouts  0.66 us

profile of v7, /device:TPU:1, one launch (start us, length us, event | category | flops | bytes accessed | tf_op | source)
XLA Modules:
  0.0 23.5 jit_solution(10199396788108872167)
XLA Ops:
  0.0 22.8 %render_exchange.1 = f32[32,8,128]{2,1,0:T(8,128)S(1)} custom-call(s32[8,16,2,8,256]{4,3,2,1,0:T(8,128)} %bitcast.8, bf16[3,256]{1,0:T(4,128)(2,1)} %colors.1, bf16[256]{0:T(256)(128)(2,1)} %opacity.1, s32[8,16]{1,0:T(8,128)} %bitcast.9), custom_call_target="tpu_custom_call" | custom-call | tf_op jit(solution)/shard_map/render_exchange/pallas_call | solution.py:300
  22.8 0.7 %copy.7 = f32[4,2,4096]{2,1,0:T(2,128)} copy(f32[4,2,4096]{2,1,0:T(2,128)S(1)} %bitcast.7) | data formatting | bytes 262144
